TPU v7x, 32 devices: a whole 2x2x4 slice. The times are simulated.
32 devices in a mesh: row: 4 (over x, core), col: 8 (over z, y).
Axes of the slice: x: 2, y: 2, z: 4, core: 2. Of those that a mesh axis runs over, the one named last changes fastest.
Arguments:
- left_factor: bfloat16 [4096, 2048], P('row', 'col'), may hold values from -6 to 6
- right_factor: bfloat16 [2048, 8192], P('row', 'col'), may hold values from -0.125 to 0.125
- matrix: float32 [4096, 8192], P('row', 'col'), may hold values from -6 to 6
- pivot_scale: float32 [2048], replicated, may hold values from 0.25 to 1.75
Outputs:
- updated: float32 [4096, 8192], P('row', 'col')
All inputs are finite; a program needn't handle non-finite values.
Results may differ from a plain program's by a relative error of at most 0.0003.
Values may be sent and summed in bfloat16 or wider, within the bound.
A program may use at most 128 MiB of HBM per device.

v0:
```python
import jax
import jax.numpy as jnp
from jax import lax
from jax.sharding import PartitionSpec as P


def taken_in(shard, axis, dim, absorb, state):
    everything = jax.tree.map(lambda a: lax.all_gather(a, axis, axis=dim, tiled=True), shard)
    return absorb(state, everything, jnp.int32(0))


def join_panel(carry, left_panel, right_panel):
    return carry + jnp.dot(left_panel, right_panel, preferred_element_type=jnp.float32)


def per_device(left_factor, right_factor, matrix, pivot_scale):
    share = left_factor.shape[1]
    part_scale = lax.dynamic_slice_in_dim(pivot_scale, lax.axis_index("col") * share, share)
    scaled_left = (left_factor.astype(jnp.float32) * part_scale).astype(jnp.bfloat16)
    begin = jnp.zeros((left_factor.shape[0], right_factor.shape[1]), jnp.float32)
    left_line = lax.all_gather(scaled_left, "col", axis=1, tiled=True)

    def take_rows(carry, piece, start):
        left_piece = lax.dynamic_slice_in_dim(left_line, start, piece.shape[0], axis=1)
        return join_panel(carry, left_piece, piece)

    total = taken_in(right_factor, "row", 0, take_rows, begin)
    updated = matrix - total
    row_power = lax.psum(jnp.sum(updated * updated, axis=1), "col")
    updated = (
        updated * lax.rsqrt(row_power / (updated.shape[1] * lax.axis_size("col")) + 1e-06)[:, None]
    )
    return updated


def solution(mesh):
    in_specs = (P("row", "col"), P("row", "col"), P("row", "col"), P())
    out_specs = P("row", "col")
    return jax.shard_map(
        per_device, mesh=mesh, in_specs=in_specs, out_specs=out_specs, check_vma=False
    )
```

profile of v0, /device:TPU:0, one launch (start us, length us, event | category | flops | bytes accessed | tf_op | source)
XLA Modules:
  0.0 170.1 jit_solution(15891152812098854044)
XLA Ops:
  6.5 0.0 all-gather.5.cloned.1.call-start
  6.5 0.7 all-gather.5.cloned.1.call-update
  7.3 0.0 all-gather.3.cloned.1.call-start
  7.3 0.8 dynamic_slice.3
  8.1 2.0 %multiply_convert_fusion = bf16[1024,256]{1,0:T(8,128)(2,1)} fusion(bf16[1024,256]{1,0:T(8,128)(2,1)} %param.4, f32[256]{0:T(256)S(1)} %dynamic_slice.3), kind=kLoop, calls=%fused_computation.3 | loop fusion | flops 786432 | bytes 1049600 | tf_op jit(solution)/shard_map/convert_element_type | solution.py:19
  10.1 0.0 all-gather.3.cloned.1.call-update
  10.1 5.3 %copy.5 = f32[1024,1024]{0,1:T(8,128)} copy(f32[1024,1024]{1,0:T(8,128)} %param.6) | data formatting | bytes 8388608 | tf_op args[2]
  15.4 30.6 %all-gather.5.cloned.1.call-done = bf16[2048,1024]{1,0:T(8,128)(2,1)} async-done(((bf16[512,1024]{1,0:T(8,128)(2,1)}), bf16[2048,1024]{1,0:T(8,128)(2,1)}) %all-gather.5.cloned.1.call-update) | async-done | bytes 4194320 | tf_op jit(solution)/shard_map/all_gather | solution.py:8
  46.0 76.8 %all-gather.3.cloned.1.call-done = bf16[1024,2048]{1,0:T(8,128)(2,1)} async-done(((bf16[1024,256]{1,0:T(8,128)(2,1)}), bf16[1024,2048]{1,0:T(8,128)(2,1)}) %all-gather.3.cloned.1.call-update) | async-done | bytes 4194320 | tf_op jit(solution)/shard_map/all_gather | solution.py:21
  122.8 11.3 %multiply_reduce_fusion = (f32[1024]{0:T(1024)S(1)}, f32[1024,1024]{0,1:T(8,128)}) fusion(f32[1024,1024]{0,1:T(8,128)} %copy.5, bf16[1024,2048]{1,0:T(8,128)(2,1)} %all-gather.3.cloned.1.call-done, bf16[2048,1024]{1,0:T(8,128)(2,1)} %all-gather.5.cloned.1.call-done), kind=kOutput, calls=%fused_computation | convolution fusion | flops 4298112000 | bytes 16781312 | tf_op jit(solution)/shard_map/dot_general | solution.py:13
  134.2 18.8 %psum.7 = f32[1024]{0:T(1024)S(1)} all-reduce(f32[1024]{0:T(1024)S(1)} %get-tuple-element.5), channel_id=1, replica_groups=mesh['row'=4,'col'=8] {'col'}, use_global_device_ids=true, to_apply=%region_1.0 | all-reduce | flops 1024 | bytes 8192 | tf_op jit(solution)/shard_map/psum | solution.py:29
  153.0 5.0 %broadcast_multiply_fusion = f32[1024,1024]{0,1:T(8,128)} fusion(f32[1024,1024]{0,1:T(8,128)} %get-tuple-element.6, f32[1024]{0:T(1024)S(1)} %add_rsqrt_fusion), kind=kLoop, calls=%fused_computation.1 | loop fusion | flops 1048576 | bytes 8392704 | tf_op jit(solution)/shard_map/mul | solution.py:31
  158.0 5.3 %copy.6 = f32[1024,1024]{1,0:T(8,128)} copy(f32[1024,1024]{0,1:T(8,128)} %broadcast_multiply_fusion) | data formatting | bytes 8388608 | tf_op jit(solution)/shard_map/mul | solution.py:31
  (1 shorter events, 0.0 us)
Async XLA Ops:
  6.5 39.5 %all-gather.5.cloned.1.call-start = ((), (), s32[]{:S(2)}) async-start(), calls=%async_computation.1 | async-start | bytes 5242880 | tf_op jit(solution)/shard_map/all_gather | solution.py:8
  7.3 115.6 %all-gather.3.cloned.1.call-start = ((), (), s32[]{:S(2)}) async-start(), calls=%async_computation | async-start | bytes 4718592 | tf_op jit(solution)/shard_map/all_gather | solution.py:21
Sparse Core Ops, SparseCore 0:
  8.9 37.0 all-gather.4
  48.1 74.7 all-gather.2
where the time goes:
time: 170 us
  waiting for transfers between devices  108 us (64%)
  blocking collectives  18.8 us (11%)
  between operations  13.4 us (8%)
  local copies, waits for them, and re-layouts  11.4 us (7%)
  matrix products  11.3 us (7%)
  other arithmetic  6.98 us (4%)
    all_gather x1, waiting for transfers between devices, per_device(): left_line = lax.all_gather(scaled_left, 'col', axis=1, tiled=True)  76.8 us
    all_gather x1, waiting for transfers between devices, taken_in(): lax.all_gather(a, axis, axis=dim, tiled=True)  30.6 us
    psum x1, blocking collectives, per_device(): row_power = lax.psum(jnp.sum(updated * updated, axis=1), 'col')  18.8 us
    dot_general x1, matrix products, join_panel(): jnp.dot(left_panel, right_panel, preferred_element_type=jnp.float32)  11.3 us
    unnamed x1, local copies, waits for them, and re-layouts  5.35 us
    mul x1, local copies, waits for them, and re-layouts, per_device(): updated * lax.rsqrt(row_power / (updated.shape[1] * lax.axis_size('col'))...  5.34 us
    mul x1, other arithmetic, per_device(): updated * lax.rsqrt(row_power / (updated.shape[1] * lax.axis_size('col'))...  4.98 us
  transfers between devices with their start and end apart: 2, of which 2 were waited for; matrix products, arithmetic and copies ran while one was open for 5% of the time, Pallas kernels for 0%

commit v1 on v0

v1 whole, which is shorter than its diff:
```python
import functools

import jax
import jax.numpy as jnp
from jax import lax
from jax.experimental import pallas as pl
from jax.experimental.pallas import tpu as pltpu
from jax.sharding import PartitionSpec as P

MESH = pl.DeviceIdType.MESH
STRIP = 128
PARTS = 4
UP, DOWN, ACROSS, RELAY = 0, 1, 2, 3


def kernel(
    n_row, n_col,
    left_hbm, right_hbm, matrix_hbm, scale_ref,
    out_ref, norm_ref,
    left, right, matrix, scaled, stats,
    left_send, left_recv, right_send, right_recv, stat_send, stat_recv, local_sem,
):
    rows, share = left_hbm.shape
    depth, cols = right_hbm.shape
    lines = n_col // 2
    strips = rows // STRIP
    part = depth // PARTS
    offset = max(lines, PARTS) - 1

    me = lax.axis_index("col")
    z, y = me // 2, me % 2
    z_pair = z + 1 - 2 * (z % 2)
    partner = z * 2 + 1 - y
    row = lax.axis_index("row")
    x, core = row // 2, row % 2
    sibling = x * 2 + 1 - core

    def strip_of(q):
        return pl.ds(pl.multiple_of(q * STRIP, STRIP), STRIP)

    def send_left(piece, q, to, way, own=False):
        return pltpu.make_async_remote_copy(
            src_ref=left_hbm.at[strip_of(q)] if own else left.at[piece, strip_of(q)],
            dst_ref=left.at[piece, strip_of(q)],
            send_sem=left_send.at[way, piece, q],
            recv_sem=left_recv.at[piece, q],
            device_id={"col": to},
            device_id_type=MESH,
        )

    def await_left(piece, q):
        send_left(piece, q, partner, ACROSS).wait_recv()

    def part_of(block, g):
        return pl.ds(pl.multiple_of(block * depth + g * part, part), part)

    def send_right(block, g, to, own=False):
        source = right_hbm.at[pl.ds(pl.multiple_of(g * part, part), part)]
        return pltpu.make_async_remote_copy(
            src_ref=source if own else right.at[part_of(block, g)],
            dst_ref=right.at[part_of(block, g)],
            send_sem=right_send.at[to, block, g],
            recv_sem=right_recv.at[block, g],
            device_id={"row": to},
            device_id_type=MESH,
        )

    def send_stat(c, to):
        return pltpu.make_async_remote_copy(
            src_ref=stats.at[me, c],
            dst_ref=stats.at[me, c],
            send_sem=stat_send.at[to, c],
            recv_sem=stat_recv.at[me, c],
            device_id={"col": to},
            device_id_type=MESH,
        )

    def await_stat(source, c):
        pltpu.make_async_remote_copy(
            src_ref=stats.at[source, c],
            dst_ref=stats.at[source, c],
            send_sem=stat_send.at[source, c],
            recv_sem=stat_recv.at[source, c],
            device_id={"col": source},
            device_id_type=MESH,
        ).wait_recv()

    own_left = pltpu.make_async_copy(left_hbm, left.at[me], local_sem.at[0])
    own_right = pltpu.make_async_copy(
        right_hbm, right.at[pl.ds(pl.multiple_of(row * depth, depth), depth)], local_sem.at[1]
    )
    own_matrix = pltpu.make_async_copy(matrix_hbm, matrix, local_sem.at[2])

    barrier = pltpu.get_barrier_semaphore()
    for step in range(1, n_col):
        pl.semaphore_signal(
            barrier, inc=1, device_id={"col": (me + step) % n_col}, device_id_type=MESH
        )
    far = [((x + step) % (n_row // 2)) * 2 + core for step in range(1, n_row // 2)]
    for other in far + [sibling]:
        pl.semaphore_signal(barrier, inc=1, device_id={"row": other}, device_id_type=MESH)
    own_left.start()
    own_right.start()
    own_matrix.start()
    pl.semaphore_wait(barrier, n_col - 1 + len(far) + 1)

    def own_sends(q, act):
        @pl.when(z < lines - 1)
        def _():
            act(send_left(me, q, me + 2, UP, own=True))

        @pl.when(z > 0)
        def _():
            act(send_left(me, q, me - 2, DOWN, own=True))

        act(send_left(me, q, partner, ACROSS, own=True))

    def passed_on(t, act, await_first):
        for d in range(1, lines):
            q = t - (d - 1)

            @pl.when((q >= 0) & (q < strips))
            def _():
                skip = (q % 2) == 1

                def cross(piece, z_from):
                    if d == 1:

                        @pl.when(jnp.logical_not((z_from == z_pair) & skip))
                        def _():
                            act(send_left(piece, q, partner, ACROSS))
                    else:
                        act(send_left(piece, q, partner, ACROSS))

                @pl.when(z + d < lines)
                def _():
                    piece = me + 2 * d
                    if await_first:
                        await_left(piece, q)

                    @pl.when(z > 0)
                    def _():
                        act(send_left(piece, q, me - 2, DOWN))

                    cross(piece, z + d)

                @pl.when(z - d >= 0)
                def _():
                    piece = me - 2 * d
                    if await_first:
                        await_left(piece, q)

                    @pl.when(z < lines - 1)
                    def _():
                        act(send_left(piece, q, me + 2, UP))

                    cross(piece, z - d)

        @pl.when((t < strips) & (t % 2 == 1))
        def _():
            if await_first:
                await_left(partner, t)
            act(send_left(partner, t, z_pair * 2 + y, RELAY))

    def start(copy):
        copy.start()

    def done(copy):
        copy.wait_send()

    @pl.loop(0, strips)
    def _(q):
        own_sends(q, start)

    @pl.loop(0, PARTS)
    def _(g):
        for other in far:
            send_right(row, g, other, own=True).start()
        send_right(row, g, sibling, own=True).start()

    def product(c):
        here = strip_of(c)
        for piece in range(n_col):
            span = slice(piece * share, (piece + 1) * share)
            scaled[:, span] = (
                left[piece, here, :].astype(jnp.float32) * scale_ref[:, span]
            ).astype(jnp.bfloat16)
        width = 256
        power = jnp.zeros((STRIP, 128), jnp.float32)

        def tile(n, power):
            span = pl.ds(pl.multiple_of(n * width, width), width)
            value = matrix[here, span] - jnp.dot(
                scaled[...], right[:, span], preferred_element_type=jnp.float32
            )
            out_ref[here, span] = value
            square = value * value
            for k in range(width // 128):
                power = power + square[:, k * 128 : (k + 1) * 128]
            return power

        power = lax.fori_loop(0, cols // width, tile, power)
        stats[me, c] = lax.dot_general(
            jnp.ones((8, 128), jnp.float32),
            power,
            (((1,), (1,)), ((), ())),
            precision=lax.Precision.HIGHEST,
            preferred_element_type=jnp.float32,
        )

    @pl.loop(0, strips + offset)
    def _(t):
        passed_on(t, start, True)

        @pl.when(t < PARTS)
        def _():
            for other in far:
                send_right(other, t, sibling).wait_recv()
                send_right(other, t, sibling).start()

        @pl.when(t == offset)
        def _():
            own_left.wait()
            own_right.wait()
            own_matrix.wait()

            @pl.loop(0, PARTS)
            def _(g):
                for step in range(n_row // 2):
                    send_right(step * 2 + 1 - core, g, sibling).wait_recv()

        c = t - offset

        @pl.when(c >= 0)
        def _():
            for line in range(lines):

                @pl.when(jnp.logical_not((line == z) & (c % 2 == 1)))
                def _():
                    await_left(line * 2 + 1 - y, c)

            product(c)
            for step in range(1, n_col):
                send_stat(c, (me + step) % n_col).start()

    @pl.loop(0, strips)
    def _(q):
        own_sends(q, done)

    @pl.loop(0, strips + lines - 2)
    def _(t):
        passed_on(t, done, False)

    @pl.loop(0, PARTS)
    def _(g):
        for other in far:
            send_right(row, g, other, own=True).wait_send()
            send_right(other, g, sibling).wait_send()
        send_right(row, g, sibling, own=True).wait_send()

    @pl.loop(0, strips)
    def _(c):
        for step in range(1, n_col):
            await_stat((me + step) % n_col, c)
            send_stat(c, (me + step) % n_col).wait_send()
        total = stats[0, c]
        for source in range(1, n_col):
            total = total + stats[source, c]
        norm_ref[c] = lax.rsqrt(total / (cols * n_col) + 1e-06)


def per_device(n_row, n_col, left_factor, right_factor, matrix, pivot_scale):
    rows, share = left_factor.shape
    depth, cols = right_factor.shape
    strips = rows // STRIP
    dma = pltpu.SemaphoreType.DMA
    updated, norm = pl.pallas_call(
        functools.partial(kernel, n_row, n_col),
        out_shape=(
            jax.ShapeDtypeStruct((rows, cols), jnp.float32),
            jax.ShapeDtypeStruct((strips, 8, STRIP), jnp.float32),
        ),
        in_specs=[pl.BlockSpec(memory_space=pl.ANY)] * 3
        + [pl.BlockSpec(memory_space=pltpu.VMEM)],
        out_specs=(
            pl.BlockSpec(memory_space=pltpu.VMEM),
            pl.BlockSpec(memory_space=pltpu.VMEM),
        ),
        scratch_shapes=[
            pltpu.VMEM((n_col, rows, share), jnp.bfloat16),
            pltpu.VMEM((n_row * depth, cols), jnp.bfloat16),
            pltpu.VMEM((rows, cols), jnp.float32),
            pltpu.VMEM((STRIP, n_col * share), jnp.bfloat16),
            pltpu.VMEM((n_col, strips, 8, STRIP), jnp.float32),
            dma((4, n_col, strips)),
            dma((n_col, strips)),
            dma((n_row, n_row, PARTS)),
            dma((n_row, PARTS)),
            dma((n_col, strips)),
            dma((n_col, strips)),
            dma((3,)),
        ],
        compiler_params=pltpu.CompilerParams(
            collective_id=0, has_side_effects=True, vmem_limit_bytes=60 * 1024 * 1024
        ),
    )(left_factor, right_factor, matrix, pivot_scale.reshape(1, -1))
    return updated * norm[:, 0, :].reshape(rows, 1)


def solution(mesh):
    in_specs = (P("row", "col"), P("row", "col"), P("row", "col"), P())
    out_specs = P("row", "col")
    body = functools.partial(per_device, mesh.shape["row"], mesh.shape["col"])
    return jax.shard_map(
        body, mesh=mesh, in_specs=in_specs, out_specs=out_specs, check_vma=False
    )
```

time: 170 us -> 74.1 us (0.44)
  waiting for transfers between devices: 108 us -> 0 us
  Pallas kernels: 0 us -> 68.6 us
  blocking collectives: 18.8 us -> 0 us
  between operations: 13.4 us -> 0.01 us
  matrix products: 11.3 us -> 0 us
  local copies, waits for them, and re-layouts: 11.4 us -> 0.76 us
  other arithmetic: 6.98 us -> 4.54 us
    all_gather x2 -> x0, waiting for transfers between devices: 107 us -> none  [the longest x1 76.8 us: per_device(): left_line = lax.all_gather(scaled_left, 'col', axis=1, tiled=True)]
    pallas_call x0 -> x1, Pallas kernels: none -> 68.6 us  [per_device(): pl.pallas_call(functools.partial(kernel, n_row, n_col), out_shape=(jax.Sh...]
    psum x1 -> x0, blocking collectives: 18.8 us -> none  [per_device(): row_power = lax.psum(jnp.sum(updated * updated, axis=1), 'col')]
    dot_general x1 -> x0, matrix products: 11.3 us -> none  [join_panel(): jnp.dot(left_panel, right_panel, preferred_element_type=jnp.float32)]
    unnamed x1 -> x0, local copies, waits for them, and re-layouts: 5.35 us -> none
    mul x1 -> x0, local copies, waits for them, and re-layouts: 5.34 us -> none  [per_device(): updated * lax.rsqrt(row_power / (updated.shape[1] * lax.axis_size('col'))...]
    convert_element_type x1 -> x0, other arithmetic: 1.99 us -> none  [per_device(): (left_factor.astype(jnp.float32) * part_scale).astype(jnp.bfloat16)]
  transfers between devices with their start and end apart: 2 -> 0, of which waited for: 2 -> 0; matrix products, arithmetic and copies ran while one was open for 5% -> 0% of each run, Pallas kernels for 0% -> 0%
where the time goes in v1:
time: 74.1 us; the launch traced here: 73.9 us
  Pallas kernels  68.6 us (93%)
  other arithmetic  4.54 us (6%)
  local copies, waits for them, and re-layouts  0.76 us (1%)
    pallas_call x1, Pallas kernels, per_device(): pl.pallas_call(functools.partial(kernel, n_row, n_col), out_shape=(jax.Sh...  68.6 us
    mul x1, other arithmetic, per_device(): return updated * norm[:, 0, :].reshape(rows, 1)  4.54 us

profile of v1, /device:TPU:0, one launch (start us, length us, event | category | flops | bytes accessed | tf_op | source)
XLA Modules:
  0.0 73.9 jit_solution(7860205149051091017)
XLA Ops:
  0.0 68.6 %shard_map.46 = (f32[1024,1024]{1,0:T(8,128)}, f32[8,8,128]{2,1,0:T(8,128)}) custom-call(bf16[1024,256]{1,0:T(8,128)(2,1)} %left_hbm.1, bf16[512,1024]{1,0:T(8,128)(2,1)} %right_hbm.1, f32[1024,1024]{1,0:T(8,128)} %matrix_hbm.1, f32[1,2048]{1,0:T(1,128)} %bitcast.3), custom_call_target="tpu_custom_call" | custom-call | tf_op jit(solution)/shard_map/pallas_call | solution.py:277
  68.6 0.8 %slice.3 = f32[8,1,128]{2,1,0:T(1,128)S(1)} slice(f32[8,8,128]{2,1,0:T(8,128)} %get-tuple-element.8), slice={[0:8], [0:1], [0:128]} | slice | bytes 8192 | tf_op jit(solution)/shard_map/slice | solution.py:307
  69.3 4.5 %broadcast_multiply_fusion = f32[1024,1024]{1,0:T(8,128)} fusion(f32[1024,1024]{1,0:T(8,128)} %get-tuple-element.7, f32[1024]{0:T(1024)S(1)} %bitcast.2), kind=kLoop, calls=%fused_computation | loop fusion | flops 1048576 | bytes 8392704 | tf_op jit(solution)/shard_map/mul | solution.py:307
